TPU v7x, 32 devices: a whole 2x2x4 slice. The times are simulated.
32 devices in a mesh: blk: 8 (over y, x, core), uly: 4 (over z).
Axes of the slice: x: 2, y: 2, z: 4, core: 2. Of those that a mesh axis runs over, the one named last changes fastest.
Arguments:
- queries: bfloat16 [4096, 4096], P(('blk', 'uly')), may hold values from -128 to 128
- keys: bfloat16 [4096, 1024], P(('blk', 'uly')), may hold values from -7 to 7
- values: bfloat16 [4096, 1024], P(('blk', 'uly')), may hold values from -6 to 6
- doc_ids: int32 [4096], P(('blk', 'uly')), may hold values from 0 to 31, never falling along the last dimension, each value on 1 to 512 neighbouring positions
- out_weight: bfloat16 [4096, 4096], P('uly'), may hold values from -0.09375 to 0.09375
Outputs:
- mixed: bfloat16 [4096, 4096], P(('blk', 'uly'))
Inputs may be any that keep to these rules, and one draw needn't show every extreme that they name: `doc_ids`: document numbers never fall along the pack; each document holds 1 to 512 consecutive tokens, and some document holds exactly 512.
All inputs are finite; a program needn't handle non-finite values.
Results may differ from a plain program's by a relative error of at most 0.017.
Values may be sent and summed in bfloat16 or wider, within the bound.
A program may use at most 64 MiB of HBM per device.

v0:
```python
import math
import jax
import jax.numpy as jnp
from jax import lax
from jax.sharding import PartitionSpec as P

HEAD_DIM = 128


def shifted(value, axis, steps):
    count = lax.axis_size(axis)
    first, last = (max(0, -steps), min(count, count - steps))
    return lax.ppermute(value, axis, [(source, source + steps) for source in range(first, last)])


def body(queries, keys, values, doc_ids, out_weight):
    n_uly = lax.axis_size("uly")
    blk_index = lax.axis_index("blk")
    rows = queries.shape[0]
    head_dim = HEAD_DIM
    heads = queries.shape[1] // head_dim
    kv_heads = keys.shape[1] // head_dim
    repeat = max(1, n_uly // kv_heads)
    kv_local = max(n_uly, kv_heads) // n_uly
    local_heads = heads // n_uly
    grouped = local_heads // kv_local
    block = rows * n_uly
    sub_rows = math.gcd(block, 512)
    n_sub = block // sub_rows
    scale = 1.0 / math.sqrt(head_dim)
    query_ids = lax.all_gather(doc_ids, "uly", axis=0, tiled=True)
    query_split = queries.reshape(rows, heads, head_dim)
    key_wide = jnp.repeat(keys.reshape(rows, kv_heads, head_dim), repeat, axis=1)
    value_wide = jnp.repeat(values.reshape(rows, kv_heads, head_dim), repeat, axis=1)
    key_wide, value_wide = (key_wide, value_wide)
    query_local, key_local, value_local = (
        lax.all_to_all(query_split, "uly", split_axis=1, concat_axis=0, tiled=True),
        lax.all_to_all(key_wide, "uly", split_axis=1, concat_axis=0, tiled=True),
        lax.all_to_all(value_wide, "uly", split_axis=1, concat_axis=0, tiled=True),
    )
    carried = (key_local, value_local)
    query_grouped = query_local.reshape(n_sub, sub_rows, kv_local, grouped, head_dim)
    query_start = blk_index * block
    query_pos = query_start + jnp.arange(block, dtype=jnp.int32)
    first_id = query_ids[0]
    offsets = jnp.arange(block, dtype=jnp.int32)
    ids_sub = query_ids.reshape(n_sub, sub_rows)
    pos_sub = query_pos.reshape(n_sub, sub_rows)

    def attend(state, pair, key_ids, source):
        key_block, value_block = pair
        key_start = jnp.maximum(source, 0) * block
        key_pos = key_start + offsets
        needed = (source >= 0) & (
            (source == blk_index) | (source < blk_index) & (key_ids[block - 1] == first_id)
        )

        def compute(state_in):

            def one(item):
                query_part, pos_part, ids_part, accum, peak, total = item
                scores = (
                    jnp.einsum(
                        "qkgd,pkd->kgqp", query_part, key_block, preferred_element_type=jnp.float32
                    )
                    * scale
                )
                allowed = (key_pos[None, :] <= pos_part[:, None]) & (
                    key_ids[None, :] == ids_part[:, None]
                )
                scores = jnp.where(allowed, scores, -1e30)
                peak_new = jnp.maximum(peak, jnp.max(scores, axis=-1))
                expo = jnp.where(allowed, jnp.exp(scores - peak_new[..., None]), 0.0)
                factor = jnp.exp(peak - peak_new)
                total_new = total * factor + jnp.sum(expo, axis=-1)
                update = jnp.einsum(
                    "kgqp,pkd->kgqd",
                    expo.astype(jnp.bfloat16),
                    value_block,
                    preferred_element_type=jnp.float32,
                )
                return (accum * factor[..., None] + update, peak_new, total_new)

            return lax.map(
                one, (query_grouped, pos_sub, ids_sub, state_in[0], state_in[1], state_in[2])
            )

        def keep(state_in):
            return state_in

        return lax.cond(needed, compute, keep, state)

    start_state = (
        jnp.zeros((n_sub, kv_local, grouped, sub_rows, head_dim), jnp.float32),
        jnp.full((n_sub, kv_local, grouped, sub_rows), -1e30, jnp.float32),
        jnp.zeros((n_sub, kv_local, grouped, sub_rows), jnp.float32),
    )
    state = attend(start_state, carried, query_ids, blk_index)
    earlier_key, earlier_value, earlier_marks = shifted(
        (carried[0], carried[1], query_ids.astype(jnp.bfloat16)), "blk", 1
    )
    earlier_ids = earlier_marks.astype(jnp.int32)
    state = attend(state, (earlier_key, earlier_value), earlier_ids, blk_index - 1)
    accum, peak, total = state
    attn = (
        (accum / total[..., None])
        .transpose(0, 3, 1, 2, 4)
        .reshape(block, local_heads * head_dim)
        .astype(jnp.bfloat16)
    )
    mixed = lax.psum_scatter(
        jnp.dot(attn, out_weight, preferred_element_type=jnp.float32).astype(jnp.bfloat16),
        "uly",
        scatter_dimension=0,
        tiled=True,
    )
    return mixed


def solution(mesh):
    placed = (
        P(("blk", "uly"), None),
        P(("blk", "uly"), None),
        P(("blk", "uly"), None),
        P(("blk", "uly")),
        P("uly", None),
    )
    return jax.shard_map(
        body, mesh=mesh, in_specs=placed, out_specs=P(("blk", "uly"), None), check_vma=False
    )
```

profile of v0, /device:TPU:0, one launch (start us, length us, event | category | flops | bytes accessed | tf_op | source)
XLA Modules:
  0.0 184.7 jit_solution(14577532152778803910)
XLA Ops:
  6.5 1.8 copy.38
  8.3 6.3 %all-to-all-start.1 = ((bf16[128,8,128]{0,2,1:T(8,128)(2,1)}), bf16[128,8,128]{0,2,1:T(8,128)(2,1)S(1)}, u32[]{:S(2)}, u32[]{:S(2)}) async-start(bf16[128,8,128]{0,2,1:T(8,128)(2,1)} %bitcast.33), calls=%async_computation.1 | async-start | bytes 524288 | tf_op jit(solution)/shard_map/all_to_all | solution.py:38
  14.7 1.8 copy.41
  16.5 7.1 %all-to-all-done.1 = bf16[128,8,128]{0,2,1:T(8,128)(2,1)S(1)} async-done(((bf16[128,8,128]{0,2,1:T(8,128)(2,1)}), bf16[128,8,128]{0,2,1:T(8,128)(2,1)S(1)}, u32[]{:S(2)}, u32[]{:S(2)}) %all-to-all-start.1) | async-done | bytes 262176 | tf_op jit(solution)/shard_map/all_to_all | solution.py:38
  23.6 3.4 %all-to-all-start.2 = ((bf16[128,8,128]{0,2,1:T(8,128)(2,1)}), bf16[128,8,128]{0,2,1:T(8,128)(2,1)S(1)}, u32[]{:S(2)}, u32[]{:S(2)}) async-start(bf16[128,8,128]{0,2,1:T(8,128)(2,1)} %bitcast.38), calls=%async_computation.2 | async-start | bytes 524288 | tf_op jit(solution)/shard_map/all_to_all | solution.py:39
  27.0 1.6 copy.34
  28.6 1.3 copy.35
  29.9 4.1 %all-to-all-done.2 = bf16[128,8,128]{0,2,1:T(8,128)(2,1)S(1)} async-done(((bf16[128,8,128]{0,2,1:T(8,128)(2,1)}), bf16[128,8,128]{0,2,1:T(8,128)(2,1)S(1)}, u32[]{:S(2)}, u32[]{:S(2)}) %all-to-all-start.2) | async-done | bytes 262176 | tf_op jit(solution)/shard_map/all_to_all | solution.py:39
  34.0 3.5 %all-to-all-start = ((bf16[128,32,128]{2,0,1:T(8,128)(2,1)}), bf16[128,32,128]{2,0,1:T(8,128)(2,1)S(1)}, u32[]{:S(2)}, u32[]{:S(2)}) async-start(bf16[128,32,128]{2,0,1:T(8,128)(2,1)} %copy.35), calls=%async_computation | async-start | bytes 2097152 | tf_op jit(solution)/shard_map/all_to_all | solution.py:37
  37.5 0.0 reduce-scatter.2.cloned.1.call-start
  37.6 0.8 copy.40
  38.4 0.9 copy.43
  39.3 1.3 collective-permute-start.1
  40.6 4.8 %collective-permute-start.2 = (bf16[512,2,128]{2,0,1:T(8,128)(2,1)}, bf16[512,2,128]{2,0,1:T(8,128)(2,1)}, u32[]{:S(2)}, u32[]{:S(2)}) collective-permute-start(bf16[512,2,128]{2,0,1:T(8,128)(2,1)} %bitcast.42), channel_id=1, source_target_pairs={{0,4},{4,8},{8,12},{12,16},{16,20},{20,24},{24,28},{1,5},{5,9},{9,... | collective-permute-start | bytes 786440 | tf_op jit(solution)/shard_map/ppermute | solution.py:13
  45.4 12.3 %all-gather = s32[4,1,128]{2,1,0:T(1,128)S(1)} all-gather(s32[1,1,128]{2,1,0:T(1,128)S(1)} %bitcast.133), channel_id=1, replica_groups=mesh['blk'=8,'uly'=4] {'uly'}, dimensions={0}, use_global_device_ids=true | all-gather | bytes 2560 | tf_op jit(solution)/shard_map/all_gather | solution.py:31
  57.7 1.3 collective-permute-start
  59.0 0.5 slice.7
  59.5 0.3 collective-permute-done
  59.8 0.6 slice.6
  61.6 0.0 all-to-all-done
  61.6 0.1 copy.37
  61.8 8.8 %conditional.2 = (f32[1,2,4,512,128]{4,3,2,1,0:T(8,128)S(1)}, f32[1,2,4,512]{3,2,1,0:T(4,128)S(1)}, f32[1,2,4,512]{3,2,1,0:T(4,128)S(1)}) conditional(s32[]{:T(128)} %convert_element_type.35, () %tuple.24, (s32[]{:T(128)}, s32[512]{0:T(512)S(1)}, s32[1,512]{1,0:T(1,128)S(1)}, s32[512]{0:T(512)S(1)}, s32[1,512]{1,0:T(1,128)S(1)}, ...), branch_computations={%region_0.0_spmd, %region_1.4_spmd} | conditional | flops 1102336512 | bytes 30093364 | solution.py:91
  61.8 0.3 compare_and_fusion
  62.1 2.5 %fusion = (f32[2,4,512]{2,1,0:T(4,128)S(1)}, f32[2,512,512,4]{2,1,3,0:T(8,128)S(1)}) fusion(pred[512,512]{0,1:T(8,128)(4,1)S(1)} %compare_and_fusion, bf16[1,512,2,4,128]{4,1,3,2,0:T(8,128)(2,1)S(1)} %get-tuple-element.136, bf16[512,2,128]{2,0,1:T(8,128)(2,1)} %get-tuple-element.134), kind=kOutput, calls=%fused_computation.2 | convolution fusion | flops 543158272 | bytes 9977856 | tf_op jit(solution)/shard_map/cond/branch_1_fun/while/body/eval_jaxpr/qkgd,pkd->kgqp/dot_general | solution.py:63
  64.6 3.9 %add_bitcast_fusion = f32[1,2,4,512,128]{4,3,2,1,0:T(8,128)S(1)} fusion(f32[2,512,512,4]{2,1,3,0:T(8,128)S(1)} %get-tuple-element.172, f32[2,4,512]{2,1,0:T(4,128)S(1)} %get-tuple-element.170, pred[512,512]{0,1:T(8,128)(4,1)S(1)} %compare_and_fusion, f32[2,4,512]{2,1,0:T(4,128)S(1)} %get-tuple-element.169, bf16[512,2,128]{2,0,1:T(8,128)(2,1)} %get-tuple-element.138), kind=kOutput, calls=%fused_computation.7 | convolution fusion | flops 547880960 | bytes 11042816 | tf_op jit(solution)/shard_map/cond/branch_1_fun/while/body/eval_jaxpr/kgqp,pkd->kgqd/dot_general | solution.py:76
  68.5 2.0 %fusion.1 = f32[2,4,512]{2,1,0:T(4,128)S(1)} fusion(f32[2,512,512,4]{2,1,3,0:T(8,128)S(1)} %get-tuple-element.172, f32[2,4,512]{2,1,0:T(4,128)S(1)} %get-tuple-element.170, pred[512,512]{0,1:T(8,128)(4,1)S(1)} %compare_and_fusion), kind=kLoop, calls=%fused_computation.3 | loop fusion | flops 10481664 | bytes 8683520 | tf_op jit(solution)/shard_map/cond/branch_1_fun/while/body/eval_jaxpr/reduce_sum | solution.py:75
  70.6 1.8 conditional.3
  70.6 1.8 copy.54
  72.4 1.9 %divide_convert_fusion = bf16[1,2,4,512,128]{3,4,2,1,0:T(8,128)(2,1)S(1)} fusion(f32[1,2,4,512,128]{3,4,2,1,0:T(8,128)} %get-tuple-element.162, f32[2,4,512]{2,1,0:T(4,128)S(1)} %bitcast.122), kind=kLoop, calls=%fused_computation.48 | loop fusion | flops 1048576 | bytes 3162112 | tf_op jit(solution)/shard_map/convert_element_type | solution.py:109
  74.3 9.5 %convolution_convert_fusion = bf16[512,4096]{1,0:T(8,128)(2,1)} fusion(bf16[512,1024]{0,1:T(8,128)(2,1)S(1)} %bitcast.119, bf16[1024,4096]{1,0:T(8,128)(2,1)} %param.13), kind=kOutput, calls=%fused_computation.47 | convolution fusion | flops 4297064448 | bytes 13631488 | tf_op jit(solution)/shard_map/dot_general | solution.py:112
  83.8 0.0 reduce-scatter.2.cloned.1.call-update
  83.8 94.0 %reduce-scatter.2.cloned.1.call-done = bf16[128,4096]{1,0:T(8,128)(2,1)} async-done(((bf16[512,4096]{1,0:T(8,128)(2,1)}), bf16[128,4096]{1,0:T(8,128)(2,1)}) %reduce-scatter.2.cloned.1.call-update) | async-done | bytes 1048592 | tf_op jit(solution)/shard_map/reduce_scatter | solution.py:111
  (12 shorter events, 0.1 us)
Async XLA Ops:
  6.5 38.9 %copy-start = (s32[128]{0:T(128)S(1)}, s32[128]{0:T(128)}, u32[]{:S(2)}) copy-start(s32[128]{0:T(128)} %param.12) | copy-start | bytes 1540
  8.3 15.3 %all-to-all-start.1 = ((bf16[128,8,128]{0,2,1:T(8,128)(2,1)}), bf16[128,8,128]{0,2,1:T(8,128)(2,1)S(1)}, u32[]{:S(2)}, u32[]{:S(2)}) async-start(bf16[128,8,128]{0,2,1:T(8,128)(2,1)} %bitcast.33), calls=%async_computation.1 | async-start | bytes 524288 | tf_op jit(solution)/shard_map/all_to_all | solution.py:38
  23.6 10.4 %all-to-all-start.2 = ((bf16[128,8,128]{0,2,1:T(8,128)(2,1)}), bf16[128,8,128]{0,2,1:T(8,128)(2,1)S(1)}, u32[]{:S(2)}, u32[]{:S(2)}) async-start(bf16[128,8,128]{0,2,1:T(8,128)(2,1)} %bitcast.38), calls=%async_computation.2 | async-start | bytes 524288 | tf_op jit(solution)/shard_map/all_to_all | solution.py:39
  34.0 27.6 %all-to-all-start = ((bf16[128,32,128]{2,0,1:T(8,128)(2,1)}), bf16[128,32,128]{2,0,1:T(8,128)(2,1)S(1)}, u32[]{:S(2)}, u32[]{:S(2)}) async-start(bf16[128,32,128]{2,0,1:T(8,128)(2,1)} %copy.35), calls=%async_computation | async-start | bytes 2097152 | tf_op jit(solution)/shard_map/all_to_all | solution.py:37
  37.5 140.3 %reduce-scatter.2.cloned.1.call-start = ((), (), s32[]{:S(2)}) async-start(), calls=%async_computation.4 | async-start | bytes 5242880 | tf_op jit(solution)/shard_map/reduce_scatter | solution.py:111
  39.3 31.3 %collective-permute-start.1 = (bf16[512,2,128]{2,0,1:T(8,128)(2,1)}, bf16[512,2,128]{2,0,1:T(8,128)(2,1)S(1)}, u32[]{:S(2)}, u32[]{:S(2)}) collective-permute-start(bf16[512,2,128]{2,0,1:T(8,128)(2,1)} %bitcast.37), channel_id=1, source_target_pairs={{0,4},{4,8},{8,12},{12,16},{16,20},{20,24},{24,28},{1,5},{5,9},{9,... | collective-permute-start | bytes 786440 | tf_op jit(solution)/shard_map/ppermute | solution.py:13
  40.6 30.0 %collective-permute-start.2 = (bf16[512,2,128]{2,0,1:T(8,128)(2,1)}, bf16[512,2,128]{2,0,1:T(8,128)(2,1)}, u32[]{:S(2)}, u32[]{:S(2)}) collective-permute-start(bf16[512,2,128]{2,0,1:T(8,128)(2,1)} %bitcast.42), channel_id=1, source_target_pairs={{0,4},{4,8},{8,12},{12,16},{16,20},{20,24},{24,28},{1,5},{5,9},{9,... | collective-permute-start | bytes 786440 | tf_op jit(solution)/shard_map/ppermute | solution.py:13
  57.7 2.1 %collective-permute-start = (bf16[512]{0:T(512)(128)(2,1)S(1)}, bf16[512]{0:T(512)(128)(2,1)S(1)}, u32[]{:S(2)}, u32[]{:S(2)}) collective-permute-start(bf16[512]{0:T(512)(128)(2,1)S(1)} %convert_element_type.32), channel_id=1, source_target_pairs={{0,4},{4,8},{8,12},{12,16},{16,20},{20,24},{24,28},{1,5},{5,9},{9,... | collective-permute-start | bytes 3080 | tf_op jit(solution)/shard_map/ppermute | solution.py:13
Sparse Core Ops, SparseCore 0:
  84.0 93.8 reduce-scatter.1
where the time goes:
time: 185 us
  waiting for transfers between devices  106 us (57%)
  starting transfers between devices  20.7 us (11%)
  matrix products  15.9 us (9%)
  between operations  14.8 us (8%)
  blocking collectives  12.3 us (7%)
  local copies, waits for them, and re-layouts  11.3 us (6%)
  other arithmetic  4.25 us (2%)
    reduce_scatter x1, waiting for transfers between devices, body(): lax.psum_scatter(jnp.dot(attn, out_weight, preferred_element_type=jnp.flo...  94 us
    all_gather x1, blocking collectives, body(): query_ids = lax.all_gather(doc_ids, 'uly', axis=0, tiled=True)  12.3 us
    dot_general x1, matrix products, body(): jnp.dot(attn, out_weight, preferred_element_type=jnp.float32)  9.49 us
    ppermute x3, starting transfers between devices, shifted(): lax.ppermute(value, axis, [(source, source + steps) for source in range(f...  7.39 us
    all_to_all x1, waiting for transfers between devices, body(): lax.all_to_all(key_wide, 'uly', split_axis=1, concat_axis=0, tiled=True)  7.13 us
    all_to_all x1, starting transfers between devices, body(): lax.all_to_all(key_wide, 'uly', split_axis=1, concat_axis=0, tiled=True)  6.35 us
    unnamed x5, local copies, waits for them, and re-layouts  5.2 us
    all_to_all x1, waiting for transfers between devices, body(): lax.all_to_all(value_wide, 'uly', split_axis=1, concat_axis=0, tiled=True)  4.06 us
  transfers between devices with their start and end apart: 7, of which 4 were waited for; matrix products, arithmetic and copies ran while one was open for 9% of the time, Pallas kernels for 0%

commit v1 on v0

--- a/solution.py
+++ b/solution.py
@@ -28,7 +28,21 @@
     sub_rows = math.gcd(block, 512)
     n_sub = block // sub_rows
     scale = 1.0 / math.sqrt(head_dim)
-    query_ids = lax.all_gather(doc_ids, "uly", axis=0, tiled=True)
+    n_chips = jax.lax.axis_size("uly")
+    series = [(to_i, (to_i + 1) % n_chips) for to_i in range(n_chips)]
+    table = [(to_i, (to_i - 1) % n_chips) for to_i in range(n_chips)]
+    mat_out, block_now = ([doc_ids], [doc_ids])
+    for _ in range(n_chips // 2):
+        big = jax.lax.ppermute(mat_out[-1], "uly", series)
+        mat_out.append(big)
+    ix = 0
+    while ix < (n_chips - 1) // 2:
+        mixed_arr = jax.lax.ppermute(block_now[-1], "uly", table)
+        block_now.append(mixed_arr)
+        ix += 1
+    extra = jnp.concatenate([*mat_out[::-1], *block_now[1:]], 0)
+    base_arr = jax.lax.axis_index("uly")
+    query_ids = jnp.roll(extra, (base_arr - n_chips // 2) * doc_ids.shape[0], 0)
     query_split = queries.reshape(rows, heads, head_dim)
     key_wide = jnp.repeat(keys.reshape(rows, kv_heads, head_dim), repeat, axis=1)
     value_wide = jnp.repeat(values.reshape(rows, kv_heads, head_dim), repeat, axis=1)

time: 185 us -> 194 us (1.049)
  waiting for transfers between devices: 106 us -> 119 us
  blocking collectives: 12.3 us -> 0 us
  starting transfers between devices: 20.7 us -> 27.9 us
    ppermute x0 -> x3, waiting for transfers between devices: none -> 16.6 us  [the longest x2 16.6 us: body(): big = jax.lax.ppermute(mat_out[-1], 'uly', series)]
    all_gather x1 -> x0, blocking collectives: 12.3 us -> none  [body(): query_ids = lax.all_gather(doc_ids, 'uly', axis=0, tiled=True)]
    ppermute x0 -> x3, starting transfers between devices: none -> 7.16 us  [the longest x2 5.21 us: body(): big = jax.lax.ppermute(mat_out[-1], 'uly', series)]
    reduce_scatter x1, waiting for transfers between devices: 94 us -> 90.7 us  [body(): lax.psum_scatter(jnp.dot(attn, out_weight, preferred_element_type=jnp.flo...]
    unnamed x5 -> x12, local copies, waits for them, and re-layouts: 5.2 us -> 5.26 us
  transfers between devices with their start and end apart: 7 -> 10, of which waited for: 4 -> 6; matrix products, arithmetic and copies ran while one was open for 9% -> 9% of each run, Pallas kernels for 0% -> 0%
where the time goes in v1:
time: 194 us; the launch traced here: 193 us
  waiting for transfers between devices  119 us (61%)
  starting transfers between devices  27.9 us (14%)
  matrix products  15.9 us (8%)
  between operations  14.8 us (8%)
  local copies, waits for them, and re-layouts  11.4 us (6%)
  other arithmetic  4.33 us (2%)
    reduce_scatter x1, waiting for transfers between devices, body(): lax.psum_scatter(jnp.dot(attn, out_weight, preferred_element_type=jnp.flo...  90.7 us
    ppermute x2, waiting for transfers between devices, body(): big = jax.lax.ppermute(mat_out[-1], 'uly', series)  16.6 us
    dot_general x1, matrix products, body(): jnp.dot(attn, out_weight, preferred_element_type=jnp.float32)  9.5 us
    ppermute x3, starting transfers between devices, shifted(): lax.ppermute(value, axis, [(source, source + steps) for source in range(f...  7.39 us
    all_to_all x1, waiting for transfers between devices, body(): lax.all_to_all(key_wide, 'uly', split_axis=1, concat_axis=0, tiled=True)  7.12 us
    all_to_all x1, starting transfers between devices, body(): lax.all_to_all(key_wide, 'uly', split_axis=1, concat_axis=0, tiled=True)  6.35 us
    unnamed x12, local copies, waits for them, and re-layouts  5.26 us
    ppermute x2, starting transfers between devices, body(): big = jax.lax.ppermute(mat_out[-1], 'uly', series)  5.21 us
  transfers between devices with their start and end apart: 10, of which 6 were waited for; matrix products, arithmetic and copies ran while one was open for 9% of the time, Pallas kernels for 0%

profile of v1, /device:TPU:0, one launch (start us, length us, event | category | flops | bytes accessed | tf_op | source)
XLA Modules:
  0.0 193.0 jit_solution(6368680779490408113)
XLA Ops:
  6.5 1.8 copy.38
  8.3 6.3 %all-to-all-start.1 = ((bf16[128,8,128]{0,2,1:T(8,128)(2,1)}), bf16[128,8,128]{0,2,1:T(8,128)(2,1)S(1)}, u32[]{:S(2)}, u32[]{:S(2)}) async-start(bf16[128,8,128]{0,2,1:T(8,128)(2,1)} %bitcast.31), calls=%async_computation.1 | async-start | bytes 524288 | tf_op jit(solution)/shard_map/all_to_all | solution.py:52
  14.7 1.8 copy.41
  16.5 7.1 %all-to-all-done.1 = bf16[128,8,128]{0,2,1:T(8,128)(2,1)S(1)} async-done(((bf16[128,8,128]{0,2,1:T(8,128)(2,1)}), bf16[128,8,128]{0,2,1:T(8,128)(2,1)S(1)}, u32[]{:S(2)}, u32[]{:S(2)}) %all-to-all-start.1) | async-done | bytes 262176 | tf_op jit(solution)/shard_map/all_to_all | solution.py:52
  23.6 3.4 %all-to-all-start.2 = ((bf16[128,8,128]{0,2,1:T(8,128)(2,1)}), bf16[128,8,128]{0,2,1:T(8,128)(2,1)S(1)}, u32[]{:S(2)}, u32[]{:S(2)}) async-start(bf16[128,8,128]{0,2,1:T(8,128)(2,1)} %bitcast.36), calls=%async_computation.2 | async-start | bytes 524288 | tf_op jit(solution)/shard_map/all_to_all | solution.py:53
  27.0 1.6 copy.34
  28.6 1.3 copy.35
  29.9 4.1 %all-to-all-done.2 = bf16[128,8,128]{0,2,1:T(8,128)(2,1)S(1)} async-done(((bf16[128,8,128]{0,2,1:T(8,128)(2,1)}), bf16[128,8,128]{0,2,1:T(8,128)(2,1)S(1)}, u32[]{:S(2)}, u32[]{:S(2)}) %all-to-all-start.2) | async-done | bytes 262176 | tf_op jit(solution)/shard_map/all_to_all | solution.py:53
  34.0 3.5 %all-to-all-start = ((bf16[128,32,128]{2,0,1:T(8,128)(2,1)}), bf16[128,32,128]{2,0,1:T(8,128)(2,1)S(1)}, u32[]{:S(2)}, u32[]{:S(2)}) async-start(bf16[128,32,128]{2,0,1:T(8,128)(2,1)} %copy.35), calls=%async_computation | async-start | bytes 2097152 | tf_op jit(solution)/shard_map/all_to_all | solution.py:51
  37.6 1.9 %collective-permute-start = (s32[128]{0:T(128)S(1)}, s32[128]{0:T(128)S(1)}, u32[]{:S(2)}, u32[]{:S(2)}) collective-permute-start(s32[128]{0:T(128)S(1)} %copy-done), channel_id=1, source_target_pairs={{0,1},{1,2},{2,3},{3,0},{4,5},{5,6},{6,7},{7,4},{8,9},{9,10},{10,1... | collective-permute-start | bytes 1544 | tf_op jit(solution)/shard_map/ppermute | solution.py:36
  39.5 1.9 %collective-permute-start.2 = (s32[128]{0:T(128)S(1)}, s32[128]{0:T(128)S(1)}, u32[]{:S(2)}, u32[]{:S(2)}) collective-permute-start(s32[128]{0:T(128)S(1)} %copy-done), channel_id=1, source_target_pairs={{0,3},{1,0},{2,1},{3,2},{4,7},{5,4},{6,5},{7,6},{8,11},{9,8},{10,9... | collective-permute-start | bytes 1544 | tf_op jit(solution)/shard_map/ppermute | solution.py:40
  41.5 14.5 %collective-permute-done = s32[128]{0:T(128)S(1)} collective-permute-done((s32[128]{0:T(128)S(1)}, s32[128]{0:T(128)S(1)}, u32[]{:S(2)}, u32[]{:S(2)}) %collective-permute-start) | collective-permute-done | bytes 544 | tf_op jit(solution)/shard_map/ppermute | solution.py:36
  56.0 3.3 %collective-permute-start.1 = (s32[128]{0:T(128)S(1)}, s32[128]{0:T(128)S(1)}, u32[]{:S(2)}, u32[]{:S(2)}) collective-permute-start(s32[128]{0:T(128)S(1)} %collective-permute-done), channel_id=1, source_target_pairs={{0,1},{1,2},{2,3},{3,0},{4,5},{5,6},{6,7},{7,4},{8,9},{9,10},{10,1... | collective-permute-start | bytes 1544 | tf_op jit(solution)/shard_map/ppermute | solution.py:36
  59.3 2.1 %collective-permute-done.1 = s32[128]{0:T(128)S(1)} collective-permute-done((s32[128]{0:T(128)S(1)}, s32[128]{0:T(128)S(1)}, u32[]{:S(2)}, u32[]{:S(2)}) %collective-permute-start.1) | collective-permute-done | bytes 544 | tf_op jit(solution)/shard_map/ppermute | solution.py:36
  61.4 0.9 copy.40
  62.3 0.9 copy.43
  63.2 1.3 collective-permute-start.4
  64.5 4.8 %collective-permute-start.5 = (bf16[512,2,128]{2,0,1:T(8,128)(2,1)}, bf16[512,2,128]{2,0,1:T(8,128)(2,1)}, u32[]{:S(2)}, u32[]{:S(2)}) collective-permute-start(bf16[512,2,128]{2,0,1:T(8,128)(2,1)} %bitcast.40), channel_id=1, source_target_pairs={{0,4},{4,8},{8,12},{12,16},{16,20},{20,24},{24,28},{1,5},{5,9},{9,... | collective-permute-start | bytes 786440 | tf_op jit(solution)/shard_map/ppermute | solution.py:13
  69.4 1.3 collective-permute-start.3
  70.7 0.6 slice.7
  71.3 0.2 collective-permute-done.3
  71.5 0.6 slice.6
  73.3 8.8 %conditional.2 = (f32[1,2,4,512,128]{4,3,2,1,0:T(8,128)S(1)}, f32[1,2,4,512]{3,2,1,0:T(4,128)S(1)}, f32[1,2,4,512]{3,2,1,0:T(4,128)S(1)}) conditional(s32[]{:T(128)} %convert_element_type.35, () %tuple.24, (s32[]{:T(128)}, s32[512]{0:T(512)S(1)}, s32[1,512]{1,0:T(1,128)S(1)}, s32[512]{0:T(512)S(1)}, s32[1,512]{1,0:T(1,128)S(1)}, ...), branch_computations={%region_0.1_spmd, %region_1.4_spmd} | conditional | flops 1102336512 | bytes 30093364 | solution.py:105
  73.4 0.3 compare_and_fusion
  73.7 2.5 %fusion = (f32[2,4,512]{2,1,0:T(4,128)S(1)}, f32[2,512,512,4]{2,1,3,0:T(8,128)S(1)}) fusion(pred[512,512]{0,1:T(8,128)(4,1)S(1)} %compare_and_fusion, bf16[1,512,2,4,128]{4,1,3,2,0:T(8,128)(2,1)S(1)} %get-tuple-element.136, bf16[512,2,128]{2,0,1:T(8,128)(2,1)} %get-tuple-element.134), kind=kOutput, calls=%fused_computation.2 | convolution fusion | flops 543158272 | bytes 9977856 | tf_op jit(solution)/shard_map/cond/branch_1_fun/while/body/eval_jaxpr/qkgd,pkd->kgqp/dot_general | solution.py:77
  76.2 3.9 %add_bitcast_fusion = f32[1,2,4,512,128]{4,3,2,1,0:T(8,128)S(1)} fusion(f32[2,512,512,4]{2,1,3,0:T(8,128)S(1)} %get-tuple-element.174, f32[2,4,512]{2,1,0:T(4,128)S(1)} %get-tuple-element.172, pred[512,512]{0,1:T(8,128)(4,1)S(1)} %compare_and_fusion, f32[2,4,512]{2,1,0:T(4,128)S(1)} %get-tuple-element.171, bf16[512,2,128]{2,0,1:T(8,128)(2,1)} %get-tuple-element.138), kind=kOutput, calls=%fused_computation.7 | convolution fusion | flops 547880960 | bytes 11042816 | tf_op jit(solution)/shard_map/cond/branch_1_fun/while/body/eval_jaxpr/kgqp,pkd->kgqd/dot_general | solution.py:90
  80.1 2.0 %fusion.1 = f32[2,4,512]{2,1,0:T(4,128)S(1)} fusion(f32[2,512,512,4]{2,1,3,0:T(8,128)S(1)} %get-tuple-element.174, f32[2,4,512]{2,1,0:T(4,128)S(1)} %get-tuple-element.172, pred[512,512]{0,1:T(8,128)(4,1)S(1)} %compare_and_fusion), kind=kLoop, calls=%fused_computation.3 | loop fusion | flops 10481664 | bytes 8683520 | tf_op jit(solution)/shard_map/cond/branch_1_fun/while/body/eval_jaxpr/reduce_sum | solution.py:89
  82.2 1.9 conditional.3
  82.2 1.8 copy.54
  84.0 1.9 divide_convert_fusion
  85.9 9.5 %convolution_convert_fusion = bf16[512,4096]{1,0:T(8,128)(2,1)} fusion(bf16[512,1024]{0,1:T(8,128)(2,1)S(1)} %bitcast.117, bf16[1024,4096]{1,0:T(8,128)(2,1)} %param.13), kind=kOutput, calls=%fused_computation.47 | convolution fusion | flops 4297064448 | bytes 13631488 | tf_op jit(solution)/shard_map/dot_general | solution.py:126
  95.5 90.7 %reduce-scatter.2.cloned.1.call-done = bf16[128,4096]{1,0:T(8,128)(2,1)} async-done(((bf16[512,4096]{1,0:T(8,128)(2,1)}), bf16[128,4096]{1,0:T(8,128)(2,1)}) %reduce-scatter.2.cloned.1.call-update) | async-done | bytes 1048592 | tf_op jit(solution)/shard_map/reduce_scatter | solution.py:125
  (26 shorter events, 0.4 us)
Async XLA Ops:
  6.5 31.1 %copy-start = (s32[128]{0:T(128)S(1)}, s32[128]{0:T(128)}, u32[]{:S(2)}) copy-start(s32[128]{0:T(128)} %param.12) | copy-start | bytes 1540
  8.3 15.3 %all-to-all-start.1 = ((bf16[128,8,128]{0,2,1:T(8,128)(2,1)}), bf16[128,8,128]{0,2,1:T(8,128)(2,1)S(1)}, u32[]{:S(2)}, u32[]{:S(2)}) async-start(bf16[128,8,128]{0,2,1:T(8,128)(2,1)} %bitcast.31), calls=%async_computation.1 | async-start | bytes 524288 | tf_op jit(solution)/shard_map/all_to_all | solution.py:52
  23.6 10.4 %all-to-all-start.2 = ((bf16[128,8,128]{0,2,1:T(8,128)(2,1)}), bf16[128,8,128]{0,2,1:T(8,128)(2,1)S(1)}, u32[]{:S(2)}, u32[]{:S(2)}) async-start(bf16[128,8,128]{0,2,1:T(8,128)(2,1)} %bitcast.36), calls=%async_computation.2 | async-start | bytes 524288 | tf_op jit(solution)/shard_map/all_to_all | solution.py:53
  34.0 39.2 %all-to-all-start = ((bf16[128,32,128]{2,0,1:T(8,128)(2,1)}), bf16[128,32,128]{2,0,1:T(8,128)(2,1)S(1)}, u32[]{:S(2)}, u32[]{:S(2)}) async-start(bf16[128,32,128]{2,0,1:T(8,128)(2,1)} %copy.35), calls=%async_computation | async-start | bytes 2097152 | tf_op jit(solution)/shard_map/all_to_all | solution.py:51
  37.5 148.6 %reduce-scatter.2.cloned.1.call-start = ((), (), s32[]{:S(2)}) async-start(), calls=%async_computation.4 | async-start | bytes 5242880 | tf_op jit(solution)/shard_map/reduce_scatter | solution.py:125
  37.6 18.4 %collective-permute-start = (s32[128]{0:T(128)S(1)}, s32[128]{0:T(128)S(1)}, u32[]{:S(2)}, u32[]{:S(2)}) collective-permute-start(s32[128]{0:T(128)S(1)} %copy-done), channel_id=1, source_target_pairs={{0,1},{1,2},{2,3},{3,0},{4,5},{5,6},{6,7},{7,4},{8,9},{9,10},{10,1... | collective-permute-start | bytes 1544 | tf_op jit(solution)/shard_map/ppermute | solution.py:36
  39.5 21.9 %collective-permute-start.2 = (s32[128]{0:T(128)S(1)}, s32[128]{0:T(128)S(1)}, u32[]{:S(2)}, u32[]{:S(2)}) collective-permute-start(s32[128]{0:T(128)S(1)} %copy-done), channel_id=1, source_target_pairs={{0,3},{1,0},{2,1},{3,2},{4,7},{5,4},{6,5},{7,6},{8,11},{9,8},{10,9... | collective-permute-start | bytes 1544 | tf_op jit(solution)/shard_map/ppermute | solution.py:40
  56.0 5.4 %collective-permute-start.1 = (s32[128]{0:T(128)S(1)}, s32[128]{0:T(128)S(1)}, u32[]{:S(2)}, u32[]{:S(2)}) collective-permute-start(s32[128]{0:T(128)S(1)} %collective-permute-done), channel_id=1, source_target_pairs={{0,1},{1,2},{2,3},{3,0},{4,5},{5,6},{6,7},{7,4},{8,9},{9,10},{10,1... | collective-permute-start | bytes 1544 | tf_op jit(solution)/shard_map/ppermute | solution.py:36
  63.2 19.0 %collective-permute-start.4 = (bf16[512,2,128]{2,0,1:T(8,128)(2,1)}, bf16[512,2,128]{2,0,1:T(8,128)(2,1)S(1)}, u32[]{:S(2)}, u32[]{:S(2)}) collective-permute-start(bf16[512,2,128]{2,0,1:T(8,128)(2,1)} %bitcast.35), channel_id=1, source_target_pairs={{0,4},{4,8},{8,12},{12,16},{16,20},{20,24},{24,28},{1,5},{5,9},{9,... | collective-permute-start | bytes 786440 | tf_op jit(solution)/shard_map/ppermute | solution.py:13
  64.5 17.7 %collective-permute-start.5 = (bf16[512,2,128]{2,0,1:T(8,128)(2,1)}, bf16[512,2,128]{2,0,1:T(8,128)(2,1)}, u32[]{:S(2)}, u32[]{:S(2)}) collective-permute-start(bf16[512,2,128]{2,0,1:T(8,128)(2,1)} %bitcast.40), channel_id=1, source_target_pairs={{0,4},{4,8},{8,12},{12,16},{16,20},{20,24},{24,28},{1,5},{5,9},{9,... | collective-permute-start | bytes 786440 | tf_op jit(solution)/shard_map/ppermute | solution.py:13
  69.4 2.1 %collective-permute-start.3 = (bf16[512]{0:T(512)(128)(2,1)S(1)}, bf16[512]{0:T(512)(128)(2,1)S(1)}, u32[]{:S(2)}, u32[]{:S(2)}) collective-permute-start(bf16[512]{0:T(512)(128)(2,1)S(1)} %get-tuple-element.165), channel_id=1, source_target_pairs={{0,4},{4,8},{8,12},{12,16},{16,20},{20,24},{24,28},{1,5},{5,9},{9,... | collective-permute-start | bytes 3080 | tf_op jit(solution)/shard_map/ppermute | solution.py:13
Sparse Core Ops, SparseCore 0:
  95.6 90.5 reduce-scatter.1
